TPU v7x, 32 devices: a whole 2x2x4 slice. The times are simulated.
32 devices in a mesh: front: 4 (over z), blk: 8 (over y, x, core).
Axes of the slice: x: 2, y: 2, z: 4, core: 2. Of those that a mesh axis runs over, the one named last changes fastest.
Arguments:
- panel_column: bfloat16 [4, 4096, 256], P('front', 'blk'), may hold values from -6 to 6
- upper_inverse: bfloat16 [4, 256, 256], P('front'), may hold values from -0.375 to 0.375
- panel_rows: bfloat16 [4, 256, 12288], P('front', None, 'blk'), may hold values from -0.375 to 0.375
- trailing: bfloat16 [4, 4096, 12288], P('front', 'blk')
- sketch: bfloat16 [12288, 256], replicated, may hold values from -0.0546875 to 0.0546875
- row_map: int32 [4, 16, 256], P('front', 'blk'), may hold values from 0 to 255, each once within a row
- parent_block: int32 [4, 16], replicated, may hold values from 0 to 23, as said below
- parent_slot: int32 [24], replicated, may hold values from 0 to 31, as said below
Outputs:
- factored_column: bfloat16 [4, 4096, 256], P('front', 'blk')
- right_factor: bfloat16 [4, 12288, 256], P('front', 'blk')
- parent_left: bfloat16 [8192, 1024], P(('front', 'blk'))
Inputs may be any that keep to these rules, and one draw needn't show every extreme that they name: `parent_block`: within one front the 16 blocks go to distinct parent blocks; some parent block receives a block of every front. `parent_slot`: distinct values: a device owns at most one parent block.
All inputs are finite; a program needn't handle non-finite values.
Results may differ from a plain program's by a relative error of at most 0.0095.
Values may be sent and summed in bfloat16 or wider, within the bound.
No kernel may reach another device: no remote copies, remote signals or barrier semaphores. Data moves between devices by JAX's collectives and lax.ppermute only.
A program may use at most 128 MiB of HBM per device.

v0:
```python
import math

import jax
import jax.numpy as jnp
from jax import lax
from jax.sharding import PartitionSpec as P


def gram_factor(sketched, slab_rows):
    local_gram = lax.dot_general(
        sketched, sketched, (((0,), (0,)), ((), ())), preferred_element_type=jnp.float32
    )
    gram_matrix = lax.psum(local_gram.astype(jnp.bfloat16), "blk").astype(jnp.float32) / slab_rows
    return jnp.linalg.cholesky(gram_matrix)


def body(
    panel_column, upper_inverse, panel_rows, trailing, sketch, row_map, parent_block, parent_slot
):
    blk_count = lax.axis_size("blk")
    front_count = lax.axis_size("front")
    front_index = lax.axis_index("front")
    block_index = lax.axis_index("blk")
    trail_local = trailing[0]
    local_rows = trail_local.shape[0]
    block_rows = row_map.shape[2]
    per_device = row_map.shape[1]
    rank_width = sketch.shape[1]
    slab_rows = local_rows * blk_count
    factored = jnp.dot(
        panel_column[0], upper_inverse[0], preferred_element_type=jnp.float32
    ).astype(jnp.bfloat16)
    window = trail_local.astype(jnp.float32)
    updated = (
        window
        - jnp.dot(
            factored,
            lax.all_gather(panel_rows, "blk", axis=2, tiled=True)[0],
            preferred_element_type=jnp.float32,
        )
    ).astype(jnp.bfloat16)
    sketched = jnp.dot(updated, sketch, preferred_element_type=jnp.float32).astype(jnp.bfloat16)
    factor_low = gram_factor(sketched, slab_rows)
    basis_rows = jax.scipy.linalg.solve_triangular(
        factor_low, sketched.astype(jnp.float32).T, lower=True
    ).T
    window = updated
    cross_share = lax.psum_scatter(
        lax.dot_general(
            window, sketched, (((0,), (0,)), ((), ())), preferred_element_type=jnp.float32
        ),
        "blk",
        scatter_dimension=0,
        tiled=True,
    )
    right_rows = jax.scipy.linalg.solve_triangular(
        factor_low, cross_share.T, lower=True
    ).T / math.sqrt(slab_rows)
    left_rows = basis_rows.astype(jnp.bfloat16).reshape(per_device, block_rows, rank_width)
    position = jnp.arange(block_rows, dtype=jnp.int32)
    permuter = (row_map[0][:, None, :] == position[None, :, None]).astype(jnp.bfloat16)
    placed = jnp.einsum(
        "bpr,brk->bpk", permuter, left_rows, preferred_element_type=jnp.float32
    ).astype(jnp.bfloat16)
    parent_count = parent_slot.shape[0]
    parent_number = jnp.arange(parent_count, dtype=jnp.int32)
    owner_all = jnp.sum(
        jnp.where(
            parent_block[:, :, None] == parent_number[None, None, :], parent_slot[None, None, :], 0
        ),
        axis=2,
    )
    block_total = owner_all.shape[1]
    device_count = front_count * blk_count
    device_number = jnp.arange(device_count, dtype=jnp.int32)
    own_owners = lax.dynamic_slice(
        owner_all, (front_index, block_index * per_device), (1, per_device)
    )[0]
    routing = (own_owners[None, :] == device_number[:, None]).astype(jnp.bfloat16)
    outgoing = jnp.einsum(
        "db,bxk->dxk", routing, placed, preferred_element_type=jnp.float32
    ).astype(jnp.bfloat16)
    incoming = lax.all_to_all(outgoing, ("front", "blk"), split_axis=0, concat_axis=0, tiled=True)
    own_slot = front_index * blk_count + block_index
    matches = owner_all == own_slot
    sources = (
        jnp.arange(front_count, dtype=jnp.int32)[:, None] * blk_count
        + jnp.arange(block_total, dtype=jnp.int32)[None, :] // per_device
    )
    selector = jnp.sum(
        jnp.logical_and(matches[:, :, None], sources[:, :, None] == device_number[None, None, :]),
        axis=1,
    ).astype(jnp.bfloat16)
    gathered = jnp.einsum(
        "fs,sxk->xfk", selector, incoming, preferred_element_type=jnp.float32
    ).astype(jnp.bfloat16)
    parent_rows = gathered.reshape(block_rows, front_count * rank_width)
    return (factored[None], right_rows.astype(jnp.bfloat16)[None], parent_rows)


def solution(mesh):
    return jax.shard_map(
        body,
        mesh=mesh,
        in_specs=(
            P("front", "blk", None),
            P("front", None, None),
            P("front", None, "blk"),
            P("front", "blk", None),
            P(),
            P("front", "blk", None),
            P(),
            P(),
        ),
        out_specs=(P("front", "blk", None), P("front", "blk", None), P(("front", "blk"), None)),
        check_vma=False,
    )
```

profile of v0, /device:TPU:0, one launch (start us, length us, event | category | flops | bytes accessed | tf_op | source)
XLA Modules:
  0.0 319.8 jit_solution(10886874956537019481)
XLA Ops:
  7.2 0.7 all-gather.2.cloned.1.call-update
  7.9 0.0 all-reduce.3.cloned.1.call-start
  8.0 0.2 copy-done
  8.1 1.1 convolution_convert_fusion.3
  9.3 48.8 %all-gather.2.cloned.1.call-done = bf16[1,256,12288]{2,1,0:T(8,128)(2,1)} async-done(((bf16[1,256,1536]{2,1,0:T(8,128)(2,1)}), bf16[1,256,12288]{2,1,0:T(8,128)(2,1)}) %all-gather.2.cloned.1.call-update) | async-done | bytes 6291472 | tf_op jit(solution)/shard_map/all_gather | solution.py:38
  58.0 10.9 %fusion = bf16[512,12288]{1,0:T(8,128)(2,1)} fusion(bf16[512,256]{1,0:T(8,128)(2,1)S(1)} %convolution_convert_fusion.3, bf16[1,512,12288]{2,1,0:T(8,128)(2,1)} %param.11, bf16[1,256,12288]{2,1,0:T(8,128)(2,1)} %all-gather.2.cloned.1.call-done), kind=kOutput, calls=%fused_computation.3 | convolution fusion | flops 3240099840 | bytes 31719424 | tf_op jit(solution)/shard_map/dot_general | solution.py:36
  68.9 9.8 %convolution_convert_fusion.1 = bf16[512,256]{1,0:T(8,128)(2,1)S(1)} fusion(bf16[512,12288]{1,0:T(8,128)(2,1)} %fusion, bf16[12288,256]{1,0:T(8,128)(2,1)} %param.12), kind=kOutput, calls=%fused_computation.12 | convolution fusion | flops 3221356544 | bytes 19136512 | tf_op jit(solution)/shard_map/dot_general | solution.py:42
  78.7 0.9 convolution_convert_fusion.4
  79.7 0.2 reduce-scatter.2.cloned.1.call-start
  79.9 12.6 %fusion.33 = f32[12288,256]{1,0:T(8,128)} fusion(bf16[512,12288]{1,0:T(8,128)(2,1)} %fusion, bf16[512,256]{1,0:T(8,128)(2,1)S(1)} %convolution_convert_fusion.1), kind=kOutput, calls=%fused_computation.74 | convolution fusion | flops 3221225472 | bytes 25427968 | tf_op jit(solution)/shard_map/dot_general | solution.py:49
  92.6 0.6 copy-done.4
  93.2 0.2 select_reduce_fusion.2
  93.4 0.1 dynamic-slice_bitcast_fusion
  93.5 39.8 %all-reduce.3.cloned.1.call-done = bf16[256,256]{0,1:T(8,128)(2,1)} async-done(((bf16[256,256]{0,1:T(8,128)(2,1)}), bf16[256,256]{0,1:T(8,128)(2,1)}) %all-reduce.3.cloned.1.call-update) | async-done | bytes 131088 | tf_op jit(solution)/shard_map/psum | solution.py:13
  133.3 0.9 convert_multiply_fusion
  134.2 0.1 copy.19
  134.3 0.9 fusion.11
  135.3 11.7 %cholesky.50 = f32[128,128]{1,0:T(8,128)S(1)} custom-call(f32[128,128]{1,0:T(8,128)S(1)} %cholesky.118), custom_call_target="Cholesky" | custom-call | tf_op jit(solution)/shard_map/jit(cholesky)/cholesky | solution.py:14
  147.1 9.8 %custom-call.18 = f32[1,128,128]{1,2,0:T(8,128)S(1)} custom-call(f32[1,128,128]{2,1,0:T(8,128)S(1)} %get-tuple-element.33), custom_call_target="InvertDiagBlocksLowerTriangular" | custom-call | tf_op jit(solution)/shard_map/jit(cholesky)/cholesky | solution.py:14
  156.9 0.2 constant_dynamic-update-slice_fusion.1
  157.1 0.3 convolution_subtract_fusion.2
  157.4 11.9 %cholesky.105 = f32[128,128]{1,0:T(8,128)S(1)} custom-call(f32[128,128]{1,0:T(8,128)S(1)} %convolution_subtract_fusion.2), custom_call_target="Cholesky" | custom-call | tf_op jit(solution)/shard_map/jit(cholesky)/cholesky | solution.py:14
  169.3 0.7 compare_reduce_fusion
  171.4 0.1 triangular_solve.74
  171.5 4.1 %while.1 = (s32[]{:T(128)}, f32[256,256]{1,0:T(8,128)S(1)}, s32[2,2]{1,0:T(2,128)S(1)}, f32[2,128,128]{2,1,0:T(8,128)S(1)}, s32[]{:T(128)}) while((s32[]{:T(128)}, f32[256,256]{1,0:T(8,128)S(1)}, s32[2,2]{1,0:T(2,128)S(1)}, f32[2,128,128]{2,1,0:T(8,128)S(1)}, s32[]{:T(128)}) %tuple.31), condition=%wide.while_cond, body=%wide.while_body.sunk | while | flops 2 | bytes 131189 | solution.py:56
  171.5 0.6 fusion.49
  172.1 1.4 bitcast_dynamic-update-slice_fusion.2
  173.5 0.6 fusion.49
  174.1 1.4 bitcast_dynamic-update-slice_fusion.2
  175.5 19.7 %custom-call.19 = f32[2,128,128]{1,2,0:T(8,128)S(1)} custom-call(f32[2,128,128]{2,1,0:T(8,128)S(1)} %get-tuple-element.10), custom_call_target="InvertDiagBlocksLowerTriangular" | custom-call | tf_op jit(solution)/shard_map/jit(_solve_triangular)/triangular_solve | solution.py:56
  195.2 0.3 fusion.32
  195.5 0.6 convolution_subtract_fusion.1
  196.1 0.4 convolution_convert_fusion.5
  196.6 0.1 copy.30
  196.7 0.2 convolution_convert_fusion.2
  197.0 1.4 convolution_convert_fusion
  198.4 4.4 %copy.24 = bf16[32,256,256]{2,1,0:T(8,128)(2,1)} copy(bf16[32,256,256]{2,0,1:T(8,128)(2,1)S(1)} %convolution_convert_fusion) | data formatting | bytes 8388608 | tf_op jit(solution)/shard_map/convert_element_type | solution.py:82
  202.7 4.4 %all-to-all-start = ((bf16[32,256,256]{2,1,0:T(8,128)(2,1)}), bf16[32,256,256]{2,1,0:T(8,128)(2,1)}, u32[]{:S(2)}, u32[]{:S(2)}) async-start(bf16[32,256,256]{2,1,0:T(8,128)(2,1)} %copy.24), calls=%async_computation.1 | async-start | bytes 8388608 | tf_op jit(solution)/shard_map/all_to_all | solution.py:83
  207.1 0.1 broadcast_add_fusion
  207.2 0.1 convert_reduce_fusion
  207.3 93.7 %all-to-all-done = bf16[32,256,256]{2,1,0:T(8,128)(2,1)} async-done(((bf16[32,256,256]{2,1,0:T(8,128)(2,1)}), bf16[32,256,256]{2,1,0:T(8,128)(2,1)}, u32[]{:S(2)}, u32[]{:S(2)}) %all-to-all-start) | async-done | bytes 4194336 | tf_op jit(solution)/shard_map/all_to_all | solution.py:83
  301.0 4.7 %fusion.5 = bf16[256,256,4]{1,2,0:T(4,128)(2,1)S(1)} fusion(bf16[32,256,256]{2,1,0:T(8,128)(2,1)} %all-to-all-done, s32[4,32]{1,0:T(4,128)S(1)} %convert_reduce_fusion), kind=kOutput, calls=%fused_computation.11 | convolution fusion | flops 17039488 | bytes 4719104 | tf_op jit(solution)/shard_map/fs,sxk->xfk/dot_general | solution.py:94
  305.7 0.9 copy.31
  306.6 2.0 fusion.9
  308.6 2.5 convolution_subtract_fusion
  311.1 0.9 fusion.21
  312.0 0.1 fusion.8
  312.1 1.2 copy.26
  (27 shorter events, 0.3 us)
Async XLA Ops:
  7.2 1.0 copy-start
  7.2 50.9 %all-gather.2.cloned.1.call-start = ((), (), s32[]{:S(2)}) async-start(), calls=%async_computation.2 | async-start | bytes 7077888 | tf_op jit(solution)/shard_map/all_gather | solution.py:38
  7.9 125.4 %all-reduce.3.cloned.1.call-start = ((), (), s32[]{:S(2)}) async-start(), calls=%async_computation.3 | async-start | bytes 262144 | tf_op jit(solution)/shard_map/psum | solution.py:13
  9.3 59.7 %copy-start.2 = (bf16[512,256]{1,0:T(8,128)(2,1)}, bf16[512,256]{1,0:T(8,128)(2,1)S(1)}, u32[]{:S(2)}) copy-start(bf16[512,256]{1,0:T(8,128)(2,1)S(1)} %convolution_convert_fusion.3) | copy-start | bytes 786436
  79.7 226.9 %reduce-scatter.2.cloned.1.call-start = ((), (), s32[]{:S(2)}) async-start(), calls=%async_computation.4 | async-start | bytes 14155776 | tf_op jit(solution)/shard_map/reduce_scatter | solution.py:48
  92.5 0.7 copy-start.4
  92.5 0.7 copy-start.5
  92.5 104.2 %copy-start.3 = (s32[1,2,256]{2,1,0:T(2,128)S(1)}, s32[1,2,256]{2,1,0:T(2,128)}, u32[]{:S(2)}) copy-start(s32[1,2,256]{2,1,0:T(2,128)} %param.13) | copy-start | bytes 6148
  202.7 98.3 %all-to-all-start = ((bf16[32,256,256]{2,1,0:T(8,128)(2,1)}), bf16[32,256,256]{2,1,0:T(8,128)(2,1)}, u32[]{:S(2)}, u32[]{:S(2)}) async-start(bf16[32,256,256]{2,1,0:T(8,128)(2,1)} %copy.24), calls=%async_computation.1 | async-start | bytes 8388608 | tf_op jit(solution)/shard_map/all_to_all | solution.py:83
  301.0 12.2 %copy-start.1 = (bf16[1,512,256]{2,1,0:T(8,128)(2,1)S(1)}, bf16[1,512,256]{2,1,0:T(8,128)(2,1)}, u32[]{:S(2)}) copy-start(bf16[1,512,256]{2,1,0:T(8,128)(2,1)} %param.8) | copy-start | bytes 786436
Sparse Core Ops, SparseCore 0:
  9.9 48.1 all-gather.1
  79.8 53.4 all-reduce.2
  136.8 130.6 reduce-scatter.1
where the time goes:
time: 320 us
  waiting for transfers between devices  183 us (57%)
  other arithmetic  56.3 us (18%)
  matrix products  48.8 us (15%)
  between operations  15.3 us (5%)
  local copies, waits for them, and re-layouts  11.7 us (4%)
  starting transfers between devices  4.66 us (1%)
    all_to_all x1, waiting for transfers between devices, body(): lax.all_to_all(outgoing, ('front', 'blk'), split_axis=0, concat_axis=0, t...  93.7 us
    all_gather x1, waiting for transfers between devices, body(): lax.all_gather(panel_rows, 'blk', axis=2, tiled=True)[0]  48.8 us
    psum x1, waiting for transfers between devices, gram_factor(): lax.psum(local_gram.astype(jnp.bfloat16), 'blk').astype(jnp.float32)  39.8 us
    another operation x6, other arithmetic, gram_factor(): return jnp.linalg.cholesky(gram_matrix)  34.2 us
    another operation x3, other arithmetic, body(): jax.scipy.linalg.solve_triangular(factor_low, cross_share.T, lower=True)  19.7 us
    dot_general x1, matrix products, body(): lax.dot_general(window, sketched, (((0,), (0,)), ((), ())), preferred_ele...  12.6 us
    dot_general x1, matrix products, body(): jnp.dot(factored, lax.all_gather(panel_rows, 'blk', axis=2, tiled=True)[0...  10.9 us
    dot_general x1, matrix products, body(): jnp.dot(updated, sketch, preferred_element_type=jnp.float32)  9.77 us
  transfers between devices with their start and end apart: 4, of which 3 were waited for; matrix products, arithmetic and copies ran while one was open for 27% of the time, Pallas kernels for 0%

commit v1 on v0

v1 whole, which is shorter than its diff:
```python
import functools
import math

import jax
import jax.numpy as jnp
from jax import lax
from jax.experimental import pallas as pl
from jax.experimental.pallas import tpu as pltpu
from jax.sharding import PartitionSpec as P


F32 = jnp.float32
BF16 = jnp.bfloat16


def fdot(a, b):
    return jnp.dot(a, b, preferred_element_type=F32)


def split_two(x):
    high = x.astype(BF16)
    return high, (x - high.astype(F32)).astype(BF16)


def dot_three(a, b):
    a_high, a_low = split_two(a)
    b_high, b_low = split_two(b)
    return fdot(a_high, b_high) + (fdot(a_high, b_low) + fdot(a_low, b_high))


VMEM = pltpu.VMEM
SMEM = pltpu.SMEM
HBM = pltpu.MemorySpace.HBM


def specs(spaces):
    return [pl.BlockSpec(memory_space=space) for space in spaces]


def local_call(kernel, spaces, out_shape, out_spaces, limit=8, **options):
    return pl.pallas_call(
        kernel,
        in_specs=specs(spaces),
        out_specs=specs(out_spaces),
        out_shape=out_shape,
        compiler_params=pltpu.CompilerParams(vmem_limit_bytes=limit << 20),
        **options,
    )


def in_hbm(x):
    return pltpu.with_memory_space_constraint(x, HBM)


def sketch_kernel(first, count, t_hbm, s_hbm, a_ref, b_ref, *refs):
    out_refs, (t_ref, s_ref, sems) = refs[:-3], refs[-3:]
    step = t_ref.shape[1] // count
    copies = []
    for i in range(count):
        near = pl.ds(i * step, step)
        far = pl.ds((first + i) * step, step)
        pair = (
            pltpu.make_async_copy(t_hbm.at[:, far], t_ref.at[:, near], sems.at[0, i]),
            pltpu.make_async_copy(s_hbm.at[far, :], s_ref.at[near, :], sems.at[1, i]),
        )
        for copy in pair:
            copy.start()
        copies.append(pair)
    if first == 0:
        factored = fdot(a_ref[...], b_ref[...]).astype(BF16)
        out_refs[1][...] = factored
        out_refs[2][...] = factored
    else:
        out_refs[0][...] = a_ref[...]
    for i in range(count):
        near = pl.ds(i * step, step)
        for copy in copies[i]:
            copy.wait()
        part = fdot(t_ref[:, near], s_ref[near, :])
        if first + i == 0:
            out_refs[0][...] = part
        else:
            out_refs[0][...] += part


def sketch_part(first, count, chunks, trail, sketch, a, b):
    rows, cols = trail.shape
    rank = sketch.shape[1]
    out_shape = [jax.ShapeDtypeStruct((rows, rank), F32)]
    if first == 0:
        out_shape += [jax.ShapeDtypeStruct((rows, b.shape[1]), BF16)] * 2
    span = cols // chunks * count
    return local_call(
        functools.partial(sketch_kernel, first, count),
        [HBM, HBM, VMEM, VMEM],
        out_shape,
        [VMEM] * len(out_shape),
        limit=24,
        scratch_shapes=[
            pltpu.VMEM((rows, span), BF16),
            pltpu.VMEM((span, rank), BF16),
            pltpu.SemaphoreType.DMA((2, count)),
        ],
    )(in_hbm(trail), in_hbm(sketch), a, b)


def in_order(core, mine, other):
    first = core == 0
    return jnp.where(first, mine, other), jnp.where(first, other, mine)


def finish_kernel(
    ts_ref, f_ref, mine_ref, other_ref, sk_ref, skt_ref, away_ref, keep_ref, work
):
    core = lax.axis_index("blk") % 2
    factored = f_ref[...]
    half = mine_ref.shape[0]
    value = ts_ref[...]
    for k, part in enumerate(in_order(core, mine_ref[...], other_ref[...])):
        high, low = split_two(part)
        columns = factored[:, k * half : (k + 1) * half]
        value = value - (fdot(columns, high) + fdot(columns, low))
    sketched = value.astype(BF16)
    sk_ref[...] = sketched
    turned = sketched.T
    skt_ref[...] = turned
    rank = sketched.shape[1]
    work[:, :rank] = fdot(turned, sketched)
    work[:, rank:] = fdot(turned, factored)
    rows = keep_ref.shape[0]
    keep_ref[...] = work[pl.ds(pl.multiple_of(core * rows, rows), rows), :]
    away_ref[...] = work[pl.ds(pl.multiple_of((1 - core) * rows, rows), rows), :]


def finish_sketch(ts, factored, mine, other):
    rows, rank = ts.shape
    wide = rank + factored.shape[1]
    return local_call(
        finish_kernel,
        [VMEM] * 4,
        [
            jax.ShapeDtypeStruct((rows, rank), BF16),
            jax.ShapeDtypeStruct((rank, rows), BF16),
            jax.ShapeDtypeStruct((rank // 2, wide), F32),
            jax.ShapeDtypeStruct((rank // 2, wide), F32),
        ],
        [VMEM] * 4,
        scratch_shapes=[pltpu.VMEM((rank, wide), F32)],
    )(ts, factored, mine, other)


def bit_of(me, mask):
    return (me // mask) % 2


def owners(me, order, stage):
    rest = order[stage + 1 :]
    base = sum(bit_of(me, mask) * mask for mask in order[:stage])
    if stage < len(order):
        base = base + (1 - bit_of(me, order[stage])) * order[stage]
    return [
        base + sum(((i >> (len(rest) - 1 - k)) & 1) * mask for k, mask in enumerate(rest))
        for i in range(1 << len(rest))
    ]


def row_base(me, order, stage, earlier):
    base = 0
    for k in range(earlier + 1, min(stage + 1, len(order))):
        bit = bit_of(me, order[k])
        base = base * 2 + (bit if k < stage else 1 - bit)
    return base * (1 << max(len(order) - stage - 1, 0))


def share_kernel(jobs, colours, skt_ref, t_hbm, *refs):
    out_refs, (t_ref, sems) = refs[: len(jobs)], refs[len(jobs) :]
    me = lax.axis_index("blk")
    width = t_ref.shape[2]
    places = []
    for out_ref, (colour, order, stage) in zip(out_refs, jobs):
        for i, owner in enumerate(owners(me, order, stage)):
            places.append((out_ref, i, owner * colours + colour))
    copies = []
    for i, (_, _, place) in enumerate(places):
        span = pl.ds(pl.multiple_of(place * width, width), width)
        copies.append(pltpu.make_async_copy(t_hbm.at[:, span], t_ref.at[i], sems.at[i]))
        copies[-1].start()
    turned = skt_ref[...]
    for i, (out_ref, at, _) in enumerate(places):
        copies[i].wait()
        out_ref[at] = fdot(turned, t_ref[i]).astype(out_ref.dtype)


def share_product(jobs, colours, skt, trail, width, dtype):
    rank, rows = skt.shape
    numbers = [1 << max(len(order) - stage - 1, 0) for _, order, stage in jobs]
    return local_call(
        functools.partial(share_kernel, jobs, colours),
        [VMEM, HBM],
        [jax.ShapeDtypeStruct((number, rank, width), dtype) for number in numbers],
        [VMEM] * len(jobs),
        limit=28,
        scratch_shapes=[
            pltpu.VMEM((sum(numbers), rows, width), BF16),
            pltpu.SemaphoreType.DMA((sum(numbers),)),
        ],
    )(skt, in_hbm(trail))


def merge_kernel(order, stage, share_ref, *refs):
    received, out_ref = refs[:-1], refs[-1]
    me = lax.axis_index("blk")
    for i in range(out_ref.shape[0]):
        total = share_ref[i]
        for t, ref in enumerate(received):
            total = total + ref[row_base(me, order, stage, t) + i].astype(F32)
        out_ref[i] = total.astype(out_ref.dtype)


def merge(order, stage, share, received):
    return local_call(
        functools.partial(merge_kernel, order, stage),
        [VMEM] * (1 + len(received)),
        [jax.ShapeDtypeStruct(share.shape, BF16)],
        [VMEM],
    )(share, *received)[0]


def early_kernel(orders, w_ref, wh_ref, p_ref, *refs):
    out_ref = refs[-1]
    me = lax.axis_index("blk")
    w_high, w_low = split_two(w_ref[...])
    wh_high, wh_low = split_two(wh_ref[...])
    at = 0
    for colour, order in enumerate(orders):
        width = refs[at].shape[2]
        total = refs[at][0]
        for t in range(len(order) - 1):
            total = total + refs[at + 1 + t][row_base(me, order, len(order), t)].astype(F32)
        at += len(order)
        high, low = split_two(total)
        own = p_ref[:, colour * width : (colour + 1) * width]
        value = fdot(w_high, high) + (fdot(w_high, low) + fdot(w_low, high))
        out_ref[colour] = value - (fdot(wh_high, own) + fdot(wh_low, own))


def right_early(orders, w, wh, panel, shares, received):
    flat = []
    for share, group in zip(shares, received):
        flat += [share] + list(group)
    rank, width = shares[0].shape[1:]
    return local_call(
        functools.partial(early_kernel, orders),
        [VMEM] * (3 + len(flat)),
        [jax.ShapeDtypeStruct((len(orders), rank, width), F32)],
        [VMEM],
        limit=16,
    )(w, wh, panel, *flat)[0]


def late_kernel(scale, w_ref, early_ref, *refs):
    last, out_ref = refs[:-1], refs[-1]
    width = early_ref.shape[2]
    w_high, w_low = split_two(w_ref[...])
    for colour, ref in enumerate(last):
        got = ref[0]
        value = early_ref[colour] + (fdot(w_high, got) + fdot(w_low, got))
        out_ref[colour * width : (colour + 1) * width, :] = (value * scale).astype(BF16).T


def right_late(w, early, last, scale):
    colours, rank, width = early.shape
    return local_call(
        functools.partial(late_kernel, scale),
        [VMEM] * (2 + len(last)),
        [jax.ShapeDtypeStruct((colours * width, rank), BF16)],
        [VMEM],
    )(w, early, *last)[0]


def spread_kernel(sk_ref, map_ref, keep_ref, send_ref, work):
    pieces, blocks, piece, _ = work.shape
    rows = pieces * piece
    me = lax.axis_index("blk")
    position = lax.broadcasted_iota(jnp.int32, (rows, rows), 0)
    for b in range(blocks):
        pick = (map_ref[b : b + 1, :] == position).astype(F32).astype(BF16)
        placed = fdot(pick, sk_ref[b * rows : (b + 1) * rows, :]).astype(BF16)
        for c in range(pieces):
            work[c, b] = placed[c * piece : (c + 1) * piece, :]
    half = pieces // 2
    for m in range(half):
        keep_ref[m] = work[jnp.bitwise_xor(me, m)]
        send_ref[m] = work[jnp.bitwise_xor(me, m + half)]


def spread_rows(sketched, row_map, pieces):
    blocks, rows = row_map.shape
    shape = (blocks, rows // pieces, sketched.shape[1])
    return local_call(
        spread_kernel,
        [VMEM, VMEM],
        [jax.ShapeDtypeStruct((pieces // 2,) + shape, BF16)] * 2,
        [VMEM] * 2,
        scratch_shapes=[pltpu.VMEM((pieces,) + shape, BF16)],
    )(sketched, row_map)


def regroup_kernel(*refs):
    keep_ref, came_ref, next_ref, send_ref = refs
    half = keep_ref.shape[0] // 2
    sources = keep_ref.shape[1]
    for m in range(half):
        for k, ref in enumerate((keep_ref, came_ref)):
            next_ref[m, k * sources : (k + 1) * sources] = ref[m]
            send_ref[m, k * sources : (k + 1) * sources] = ref[m + half]


def regroup(keep, came):
    half, sources = keep.shape[0] // 2, 2 * keep.shape[1]
    shape = jax.ShapeDtypeStruct((half, sources) + keep.shape[2:], BF16)
    return local_call(regroup_kernel, [VMEM] * 2, [shape] * 2, [VMEM] * 2)(keep, came)


def route_kernel(source_ref, w_ref, *refs):
    spread, (out_ref, work) = refs[:-2], refs[-2:]
    _, blocks, piece, rank = spread[0].shape
    w_high, w_low = split_two(w_ref[...])
    rows = jnp.concatenate([ref[0].reshape(blocks * piece, rank) for ref in spread], axis=0)
    across = (((1,), (1,)), ((), ()))
    value = lax.dot_general(rows, w_high, across, preferred_element_type=F32)
    value = value + lax.dot_general(rows, w_low, across, preferred_element_type=F32)
    work[0] = jnp.zeros((piece, rank), BF16)
    for b in range(blocks * len(spread)):
        work[1 + b] = value[b * piece : (b + 1) * piece, :].astype(BF16)

    def move(d, carry):
        out_ref[d] = work[source_ref[d]]
        return carry

    lax.fori_loop(0, out_ref.shape[0], move, 0, unroll=4)


def route_left(source, spread, w):
    _, blocks, piece, rank = spread[0].shape
    return local_call(
        route_kernel,
        [SMEM, VMEM] + [VMEM] * len(spread),
        [jax.ShapeDtypeStruct((source.shape[0], piece, rank), BF16)],
        [VMEM],
        scratch_shapes=[pltpu.VMEM((blocks * len(spread) + 1, piece, rank), BF16)],
    )(source, w, *spread)[0]


def gather_kernel(x_ref, out_ref):
    devices, piece, rank = x_ref.shape
    pieces = out_ref.shape[0] // piece
    for d in range(devices):
        f, c = d // pieces, d % pieces
        out_ref[c * piece : (c + 1) * piece, f * rank : (f + 1) * rank] = x_ref[d]


def gather_left(x, fronts):
    devices, piece, rank = x.shape
    return local_call(
        gather_kernel,
        [VMEM],
        [jax.ShapeDtypeStruct((devices // fronts * piece, fronts * rank), BF16)],
        [VMEM],
    )(x)[0]


TILE = 8
LANES = 128


def eliminate(tiles, pivots):
    tiles = list(tiles)
    count = len(tiles)
    row = lax.broadcasted_iota(jnp.int32, (TILE, LANES), 0)
    group = TILE
    for start in range(0, pivots, group):
        home = start // TILE
        at = start % TILE
        col = [
            {
                t: jnp.broadcast_to(tiles[t][:, start + b : start + b + 1], (TILE, LANES))
                for t in range(home, count)
            }
            for b in range(group)
        ]
        rows = [tiles[home][at + a : at + a + 1, :] for a in range(group)]
        entry = [
            [col[b][home][at + a : at + a + 1, :] for b in range(a + 1)] for a in range(group)
        ]
        low = [[None] * group for _ in range(group)]
        inv = [[None] * group for _ in range(group)]
        for b in range(group):
            pivot = entry[b][b]
            for c in range(b):
                pivot = pivot - low[b][c] * low[b][c]
            root = lax.rsqrt(pivot)
            inv[b][b] = root
            for a in range(b + 1, group):
                value = entry[a][b]
                for c in range(b):
                    value = value - low[a][c] * low[b][c]
                low[a][b] = value * root
        for a in range(group):
            for b in range(a):
                value = low[a][b] * inv[b][b]
                for c in range(b + 1, a):
                    value = value + low[a][c] * inv[c][b]
                inv[a][b] = -(inv[a][a] * value)
        scaled = []
        for a in range(group):
            value = inv[a][0] * rows[0]
            for b in range(1, a + 1):
                value = value + inv[a][b] * rows[b]
            scaled.append(value)
        for t in range(home, count):
            if t == home and at + group == TILE:
                new = tiles[t]
            else:
                new = tiles[t]
                for a in range(group):
                    factor = inv[a][0] * col[0][t]
                    for b in range(1, a + 1):
                        factor = factor + inv[a][b] * col[b][t]
                    new = new - factor * scaled[a]
                if t == home:
                    new = jnp.where(row >= at + group, new, tiles[t])
            if t == home:
                for a in range(group):
                    new = jnp.where(row == at + a, scaled[a], new)
            tiles[t] = new
    return tiles


def factor_kernel(scale, nb, mine_ref, other_ref, w_ref, wh_ref, work, side):
    size = w_ref.shape[0]
    half = size // 2
    for k, part in enumerate(in_order(lax.axis_index("blk") % 2, mine_ref[...], other_ref[...])):
        work[k * half : (k + 1) * half, :size] = part[:, :size] * scale
        side[k * half : (k + 1) * half, :] = part[:, size:]
    row = lax.broadcasted_iota(jnp.int32, (size, size), 0)
    col = lax.broadcasted_iota(jnp.int32, (size, size), 1)
    work[:, size:] = (row == col).astype(F32)
    small_row = lax.broadcasted_iota(jnp.int32, (nb, nb), 0)
    small_col = lax.broadcasted_iota(jnp.int32, (nb, nb), 1)
    unit = (small_row == small_col).astype(F32)
    for k in range(size // nb):
        low, high = k * nb, (k + 1) * nb
        both = jnp.concatenate([work[low:high, low:high], unit], axis=1)
        tiles = eliminate([both[t * TILE : (t + 1) * TILE, :] for t in range(nb // TILE)], nb)
        own = jnp.concatenate(tiles, axis=0)[:, nb : 2 * nb]
        wide = dot_three(own, work[low:high, :])
        w_ref[low:high, :] = wide[:, size:]
        if high < size:
            left = wide[:, high:size].T
            work[high:, :] = work[high:, :] - dot_three(left, wide)
    wh_ref[...] = dot_three(w_ref[...], side[...])


def factor_inverse(mine, other, scale):
    size = 2 * mine.shape[0]
    rest = mine.shape[1] - size
    return local_call(
        functools.partial(factor_kernel, scale, LANES // 2),
        [VMEM, VMEM],
        [jax.ShapeDtypeStruct((size, size), F32), jax.ShapeDtypeStruct((size, rest), F32)],
        [VMEM, VMEM],
        scratch_shapes=[pltpu.VMEM((size, 2 * size), F32), pltpu.VMEM((size, rest), F32)],
    )(mine, other)


def flip(x, masks):
    return lax.ppermute(x, "blk", [(i, i ^ m) for i, m in enumerate(masks)])


def sum_steps(total):
    bits = [1 << k for k in range(1, total.bit_length() - 1)]
    return [
        [bits[k] if i % 2 == 0 else bits[-1 - k] for i in range(total)] for k in range(len(bits))
    ]


def body(
    panel_column, upper_inverse, panel_rows, trailing, sketch, row_map, parent_block, parent_slot
):
    blk_count = lax.axis_size("blk")
    front_count = lax.axis_size("front")
    front_index = lax.axis_index("front")
    me = lax.axis_index("blk")
    trail = trailing[0]
    rows, cols = trail.shape
    per_device = row_map.shape[1]
    slab_rows = rows * blk_count
    own_cols = cols // blk_count
    own_panel = panel_rows[0]

    cores = [1] * blk_count
    steps = sum_steps(blk_count)

    own_sketch = lax.dynamic_slice_in_dim(sketch, me * own_cols, own_cols, 0)
    local = fdot(own_panel, own_sketch)
    half = local.shape[0] // 2
    away = lax.dynamic_slice_in_dim(local, (1 - me % 2) * half, half, 0)
    mine = lax.dynamic_slice_in_dim(local, (me % 2) * half, half, 0)
    came = flip(away, cores)
    mine = mine + came
    for step in steps:
        came = flip(mine, step)
        mine = mine + came
    other = flip(mine, cores)
    chunks = 8
    trail_sketch, kept, factored = sketch_part(
        0, chunks // 2, chunks, trail, sketch, panel_column[0], upper_inverse[0]
    )
    trail_sketch = sketch_part(
        chunks // 2, chunks // 2, chunks, trail, sketch, trail_sketch, kept
    )[0]
    sketched, turned, away, mine = finish_sketch(trail_sketch, kept, mine, other)

    colours = 2 if own_cols % (2 * LANES) == 0 else 1
    width = own_cols // colours
    others = [1 << k for k in range(1, blk_count.bit_length() - 1)]
    orders = [[1] + others, [1] + others[::-1]][:colours]
    stages = len(orders[0])
    came = flip(away, cores)
    mine = mine + came
    received = []
    jobs = [(colour, order, 0) for colour, order in enumerate(orders)]
    sent = share_product(jobs, colours, turned, trail, width, BF16)
    for colour in range(colours):
        received.append([flip(sent[colour], cores)])
    shares = [[] for _ in orders]
    for wanted in ([1], list(range(2, stages + 1))):
        jobs = [(c, order, stage) for c, order in enumerate(orders) for stage in wanted]
        got = share_product(jobs, colours, turned, trail, width, F32)
        for (colour, _, _), share in zip(jobs, got):
            shares[colour].append(share)
    kept_rows, away_rows = spread_rows(sketched, row_map[0], blk_count)
    kept_rows, away_rows = kept_rows[:, None], away_rows[:, None]
    reach = blk_count // 2
    distances = [0]
    while True:
        came_rows = flip(away_rows, [reach] * blk_count)
        if reach == 1:
            break
        kept_rows, away_rows = regroup(kept_rows, came_rows)
        distances += [d + reach for d in distances]
        reach //= 2
    distances += [d + 1 for d in distances]
    spread = [x.reshape((1, -1) + x.shape[3:]) for x in (kept_rows, came_rows)]
    for step in steps:
        came = flip(mine, step)
        mine = mine + came
    other = flip(mine, cores)

    def exchange(stage):
        for colour, order in enumerate(orders):
            sent = merge(order, stage, shares[colour][stage - 1], received[colour])
            received[colour].append(flip(sent, [order[stage]] * blk_count))

    exchange(1)
    inverse, inverse_products = factor_inverse(mine, other, 1.0 / slab_rows)

    parent_number = jnp.arange(parent_slot.shape[0], dtype=jnp.int32)
    own_blocks = lax.dynamic_index_in_dim(parent_block, front_index, 0, keepdims=False)
    owner = jnp.sum(
        jnp.where(own_blocks[:, None] == parent_number[None, :], parent_slot[None, :], 0), axis=1
    )
    device_number = jnp.arange(front_count * blk_count, dtype=jnp.int32)
    block_number = jnp.arange(blk_count * per_device, dtype=jnp.int32)
    rank_of = [distances.index(d) for d in range(blk_count)]
    distance = jnp.bitwise_xor(block_number // per_device, me)
    place = jnp.sum(
        jnp.where(
            distance[:, None] == jnp.arange(blk_count, dtype=jnp.int32)[None, :],
            jnp.array(rank_of, jnp.int32)[None, :],
            0,
        ),
        axis=1,
    )
    block_number = place * per_device + block_number % per_device + 1
    source = jnp.sum(
        jnp.where(owner[None, :] == device_number[:, None], block_number[None, :], 0), axis=1
    ).astype(jnp.int32)
    outgoing = route_left(source, spread, inverse)
    incoming = lax.all_to_all(outgoing, ("front", "blk"), 0, 0, tiled=True)

    for stage in range(2, stages):
        exchange(stage)
    early = right_early(
        orders,
        inverse,
        inverse_products,
        own_panel,
        [share[-1] for share in shares],
        [group[:-1] for group in received],
    )
    right = right_late(
        inverse, early, [group[-1] for group in received], 1.0 / math.sqrt(slab_rows)
    )
    parent_rows = gather_left(incoming, front_count)
    return (factored[None], right[None], parent_rows)


def solution(mesh):
    return jax.shard_map(
        body,
        mesh=mesh,
        in_specs=(
            P("front", "blk", None),
            P("front", None, None),
            P("front", None, "blk"),
            P("front", "blk", None),
            P(),
            P("front", "blk", None),
            P(),
            P(),
        ),
        out_specs=(
            P("front", "blk", None),
            P("front", "blk", None),
            P(("front", "blk"), None),
        ),
        check_vma=False,
    )
```

time: 320 us -> 108 us (0.34)
  waiting for transfers between devices: 183 us -> 22.1 us
  other arithmetic: 56.3 us -> 2.25 us
  Pallas kernels: 0 us -> 49 us
  matrix products: 48.8 us -> 1.79 us
  starting transfers between devices: 4.66 us -> 26.2 us
  between operations: 15.3 us -> 0.95 us
  local copies, waits for them, and re-layouts: 11.7 us -> 5.47 us
    all_to_all x1, waiting for transfers between devices: 93.7 us -> 4.88 us  [body(): incoming = lax.all_to_all(outgoing, ('front', 'blk'), 0, 0, tiled=True)]
    another operation x9 -> x0, other arithmetic: 53.9 us -> none  [the longest x6 34.2 us: gram_factor(): return jnp.linalg.cholesky(gram_matrix)]
    pallas_call x0 -> x18, Pallas kernels: none -> 49 us  [the longest x3 11.7 us: share_product(): local_call(functools.partial(share_kernel, jobs, colours), [VMEM, HBM], [...]
    all_gather x1 -> x0, waiting for transfers between devices: 48.8 us -> none  [body(): lax.all_gather(panel_rows, 'blk', axis=2, tiled=True)[0]]
    dot_general x8 -> x1, matrix products: 41.6 us -> 1.79 us  [fdot(): return jnp.dot(a, b, preferred_element_type=F32)]
    psum x1 -> x0, waiting for transfers between devices: 39.8 us -> none  [gram_factor(): lax.psum(local_gram.astype(jnp.bfloat16), 'blk').astype(jnp.float32)]
    ppermute x0 -> x17, starting transfers between devices: none -> 22.1 us  [flip(): return lax.ppermute(x, 'blk', [(i, i ^ m) for i, m in enumerate(masks)])]
    ppermute x0 -> x17, waiting for transfers between devices: none -> 17.2 us  [flip(): return lax.ppermute(x, 'blk', [(i, i ^ m) for i, m in enumerate(masks)])]
  transfers between devices with their start and end apart: 4 -> 18, of which waited for: 3 -> 7; matrix products, arithmetic and copies ran while one was open for 27% -> 2% of each run, Pallas kernels for 0% -> 37%
where the time goes in v1:
time: 108 us
  Pallas kernels  49 us (45%)
  starting transfers between devices  26.2 us (24%)
  waiting for transfers between devices  22.1 us (20%)
  local copies, waits for them, and re-layouts  5.47 us (5%)
  other arithmetic  2.25 us (2%)
  matrix products  1.79 us (2%)
    ppermute x17, starting transfers between devices, flip(): return lax.ppermute(x, 'blk', [(i, i ^ m) for i, m in enumerate(masks)])  22.1 us
    ppermute x17, waiting for transfers between devices, flip(): return lax.ppermute(x, 'blk', [(i, i ^ m) for i, m in enumerate(masks)])  17.2 us
    pallas_call x3, Pallas kernels, share_product(): local_call(functools.partial(share_kernel, jobs, colours), [VMEM, HBM], [...  11.7 us
    pallas_call x2, Pallas kernels, sketch_part(): local_call(functools.partial(sketch_kernel, first, count), [HBM, HBM, VME...  10.6 us
    pallas_call x1, Pallas kernels, factor_inverse(): local_call(functools.partial(factor_kernel, scale, LANES // 2), [VMEM, VM...  9.14 us
    pallas_call x4, Pallas kernels, merge(): local_call(functools.partial(merge_kernel, order, stage), [VMEM] * (1 + l...  6.66 us
    unnamed x32, local copies, waits for them, and re-layouts  5.45 us
    all_to_all x1, waiting for transfers between devices, body(): incoming = lax.all_to_all(outgoing, ('front', 'blk'), 0, 0, tiled=True)  4.88 us
  transfers between devices with their start and end apart: 18, of which 7 were waited for; matrix products, arithmetic and copies ran while one was open for 2% of the time, Pallas kernels for 37%

profile of v1, /device:TPU:0, one launch (start us, length us, event | category | flops | bytes accessed | tf_op | source)
XLA Modules:
  0.0 107.7 jit_solution(13062051513961512968)
XLA Ops:
  0.7 1.8 %fusion = f32[256,256]{0,1:T(8,128)S(1)} fusion(bf16[12288,256]{1,0:T(8,128)(2,1)} %s_hbm.3, s32[]{:T(128)S(6)} %select_n.53, bf16[1,256,1536]{2,1,0:T(8,128)(2,1)} %param.11), kind=kOutput, calls=%fused_computation | convolution fusion | flops 201326592 | bytes 1835012 | tf_op jit(solution)/shard_map/dot_general | solution.py:17
  2.5 0.6 collective-permute-start
  3.1 1.0 collective-permute-done
  4.1 2.9 %collective-permute-start.1 = (f32[128,256]{1,0:T(8,128)S(1)}, f32[128,256]{1,0:T(8,128)S(1)}, u32[]{:S(2)}, u32[]{:S(2)}) collective-permute-start(f32[128,256]{1,0:T(8,128)S(1)} %bitcast_add_fusion), channel_id=1, source_target_pairs={{0,2},{1,5},{2,0},{3,7},{4,6},{5,1},{6,4},{7,3},{8,10},{9,13},{10,... | collective-permute-start | bytes 393224 | tf_op jit(solution)/shard_map/ppermute | solution.py:478
  7.0 2.9 %collective-permute-done.1 = f32[128,256]{1,0:T(8,128)S(1)} collective-permute-done((f32[128,256]{1,0:T(8,128)S(1)}, f32[128,256]{1,0:T(8,128)S(1)}, u32[]{:S(2)}, u32[]{:S(2)}) %collective-permute-start.1) | collective-permute-done | bytes 131104 | tf_op jit(solution)/shard_map/ppermute | solution.py:478
  9.9 2.1 %collective-permute-start.2 = (f32[128,256]{1,0:T(8,128)S(1)}, f32[128,256]{1,0:T(8,128)S(1)}, u32[]{:S(2)}, u32[]{:S(2)}) collective-permute-start(f32[128,256]{1,0:T(8,128)S(1)} %add.70), channel_id=1, source_target_pairs={{0,4},{1,3},{2,6},{3,1},{4,0},{5,7},{6,2},{7,5},{8,12},{9,11},{10,... | collective-permute-start | bytes 393224 | tf_op jit(solution)/shard_map/ppermute | solution.py:478
  12.1 2.9 %collective-permute-done.2 = f32[128,256]{1,0:T(8,128)S(1)} collective-permute-done((f32[128,256]{1,0:T(8,128)S(1)}, f32[128,256]{1,0:T(8,128)S(1)}, u32[]{:S(2)}, u32[]{:S(2)}) %collective-permute-start.2) | collective-permute-done | bytes 131104 | tf_op jit(solution)/shard_map/ppermute | solution.py:478
  15.1 5.3 %shard_map.112 = (f32[512,256]{1,0:T(8,128)S(1)}, bf16[512,256]{1,0:T(8,128)(2,1)S(1)}, bf16[512,256]{1,0:T(8,128)(2,1)}) custom-call(bf16[512,12288]{1,0:T(8,128)(2,1)} %bitcast.27, bf16[12288,256]{1,0:T(8,128)(2,1)} %s_hbm.3, bf16[512,256]{1,0:T(8,128)(2,1)S(1)} %bitcast.20, bf16[256,256]{1,0:T(8,128)(2,1)S(1)} %bitcast.21), custom_call_target="tpu_custom_call" | custom-call | tf_op jit(solution)/shard_map/pallas_call | solution.py:93
  20.4 5.3 %shard_map.113.ts_ref = f32[512,256]{1,0:T(8,128)S(1)} custom-call(bf16[512,12288]{1,0:T(8,128)(2,1)} %bitcast.28, bf16[12288,256]{1,0:T(8,128)(2,1)} %s_hbm.3, f32[512,256]{1,0:T(8,128)S(1)} %get-tuple-element.27.a_ref, bf16[512,256]{1,0:T(8,128)(2,1)S(1)} %get-tuple-element.28.b_ref.f_ref), custom_call_target="tpu_custom_call" | custom-call | tf_op jit(solution)/shard_map/pallas_call | solution.py:93
  25.7 0.8 shard_map.114
  26.5 5.9 %shard_map.117 = (bf16[4,256,768]{2,1,0:T(8,128)(2,1)}, bf16[4,256,768]{2,1,0:T(8,128)(2,1)}) custom-call(bf16[256,512]{1,0:T(8,128)(2,1)S(1)} %get-tuple-element.33.skt_ref, bf16[512,12288]{1,0:T(8,128)(2,1)} %bitcast.29), custom_call_target="tpu_custom_call" | custom-call | tf_op jit(solution)/shard_map/pallas_call | solution.py:197
  32.4 0.5 collective-permute-start.10
  33.0 0.4 collective-permute-start.4
  33.5 5.4 %collective-permute-done.4 = f32[128,512]{1,0:T(8,128)S(1)} collective-permute-done((f32[128,512]{1,0:T(8,128)S(1)}, f32[128,512]{1,0:T(8,128)S(1)}, u32[]{:S(2)}, u32[]{:S(2)}) %collective-permute-start.4) | collective-permute-done | bytes 262176 | tf_op jit(solution)/shard_map/ppermute | solution.py:478
  38.9 2.1 %collective-permute-start.5 = (f32[128,512]{1,0:T(8,128)S(1)}, f32[128,512]{1,0:T(8,128)S(1)}, u32[]{:S(2)}, u32[]{:S(2)}) collective-permute-start(f32[128,512]{1,0:T(8,128)S(1)} %add.72), channel_id=1, source_target_pairs={{0,2},{1,5},{2,0},{3,7},{4,6},{5,1},{6,4},{7,3},{8,10},{9,13},{10,... | collective-permute-start | bytes 786440 | tf_op jit(solution)/shard_map/ppermute | solution.py:478
  41.2 1.6 %collective-permute-start.14 = (bf16[4,1,2,32,256]{4,3,2,1,0:T(8,128)(2,1)S(1)}, bf16[4,1,2,32,256]{4,3,2,1,0:T(8,128)(2,1)S(1)}, u32[]{:S(2)}, u32[]{:S(2)}) collective-permute-start(bf16[4,1,2,32,256]{4,3,2,1,0:T(8,128)(2,1)S(1)} %bitcast.26), channel_id=1, source_target_pairs={{0,4},{1,5},{2,6},{3,7},{4,0},{5,1},{6,2},{7,3},{8,12},{9,13},{10,... | collective-permute-start | bytes 393224 | tf_op jit(solution)/shard_map/ppermute | solution.py:478
  42.8 2.5 %collective-permute-done.5 = f32[128,512]{1,0:T(8,128)S(1)} collective-permute-done((f32[128,512]{1,0:T(8,128)S(1)}, f32[128,512]{1,0:T(8,128)S(1)}, u32[]{:S(2)}, u32[]{:S(2)}) %collective-permute-start.5) | collective-permute-done | bytes 262176 | tf_op jit(solution)/shard_map/ppermute | solution.py:478
  45.3 0.7 add.73
  46.0 2.0 %collective-permute-start.6 = (f32[128,512]{1,0:T(8,128)}, f32[128,512]{1,0:T(8,128)}, u32[]{:S(2)}, u32[]{:S(2)}) collective-permute-start(f32[128,512]{1,0:T(8,128)} %add.73), channel_id=1, source_target_pairs={{0,4},{1,3},{2,6},{3,1},{4,0},{5,7},{6,2},{7,5},{8,12},{9,11},{10,... | collective-permute-start | bytes 786440 | tf_op jit(solution)/shard_map/ppermute | solution.py:478
  48.2 0.7 shard_map.126
  48.8 1.5 %collective-permute-start.15 = (bf16[2,2,2,32,256]{4,3,2,1,0:T(8,128)(2,1)}, bf16[2,2,2,32,256]{4,3,2,1,0:T(8,128)(2,1)}, u32[]{:S(2)}, u32[]{:S(2)}) collective-permute-start(bf16[2,2,2,32,256]{4,3,2,1,0:T(8,128)(2,1)} %get-tuple-element.46), channel_id=1, source_target_pairs={{0,2},{1,3},{2,0},{3,1},{4,6},{5,7},{6,4},{7,5},{8,10},{9,11},{10,... | collective-permute-start | bytes 393224 | tf_op jit(solution)/shard_map/ppermute | solution.py:478
  50.3 2.4 %collective-permute-done.6 = f32[128,512]{1,0:T(8,128)} collective-permute-done((f32[128,512]{1,0:T(8,128)}, f32[128,512]{1,0:T(8,128)}, u32[]{:S(2)}, u32[]{:S(2)}) %collective-permute-start.6) | collective-permute-done | bytes 262176 | tf_op jit(solution)/shard_map/ppermute | solution.py:478
  52.7 1.1 add.74.mine_ref
  53.9 2.9 %shard_map.118 = (f32[2,256,768]{2,1,0:T(8,128)S(1)}, f32[2,256,768]{2,1,0:T(8,128)S(1)}) custom-call(bf16[256,512]{1,0:T(8,128)(2,1)S(1)} %get-tuple-element.33.skt_ref, bf16[512,12288]{1,0:T(8,128)(2,1)} %bitcast.30), custom_call_target="tpu_custom_call" | custom-call | tf_op jit(solution)/shard_map/pallas_call | solution.py:197
  56.8 0.9 shard_map.127
  57.8 0.5 collective-permute-start.16
  58.3 1.0 shard_map.120
  59.3 2.0 %collective-permute-start.11 = (bf16[2,256,768]{2,1,0:T(8,128)(2,1)}, bf16[2,256,768]{2,1,0:T(8,128)(2,1)}, u32[]{:S(2)}, u32[]{:S(2)}) collective-permute-start(bf16[2,256,768]{2,1,0:T(8,128)(2,1)} %shard_map.120), channel_id=1, source_target_pairs={{0,4},{1,5},{2,6},{3,7},{4,0},{5,1},{6,2},{7,3},{8,12},{9,13},{10,... | collective-permute-start | bytes 2359304 | tf_op jit(solution)/shard_map/ppermute | solution.py:478
  61.3 1.1 shard_map.119
  62.4 2.4 %collective-permute-start.9 = (bf16[2,256,768]{2,1,0:T(8,128)(2,1)}, bf16[2,256,768]{2,1,0:T(8,128)(2,1)}, u32[]{:S(2)}, u32[]{:S(2)}) collective-permute-start(bf16[2,256,768]{2,1,0:T(8,128)(2,1)} %shard_map.119), channel_id=1, source_target_pairs={{0,2},{1,3},{2,0},{3,1},{4,6},{5,7},{6,4},{7,5},{8,10},{9,11},{10,... | collective-permute-start | bytes 2359304 | tf_op jit(solution)/shard_map/ppermute | solution.py:478
  65.1 9.1 %shard_map.115 = (f32[256,256]{1,0:T(8,128)S(1)}, f32[256,256]{1,0:T(8,128)S(1)}) custom-call(f32[128,512]{1,0:T(8,128)S(1)} %add.74.mine_ref, f32[128,512]{1,0:T(8,128)S(1)} %collective-permute-done.7.other_ref), custom_call_target="tpu_custom_call" | custom-call | tf_op jit(solution)/shard_map/pallas_call | solution.py:468
  74.2 0.7 copy-done.10
  74.9 0.9 shard_map.128
  75.9 0.7 copy-done.2
  76.6 0.8 copy-done.4
  77.4 4.1 %all-to-all-start = ((bf16[32,32,256]{2,1,0:T(8,128)(2,1)}), bf16[32,32,256]{2,1,0:T(8,128)(2,1)}, u32[]{:S(2)}, u32[]{:S(2)}) async-start(bf16[32,32,256]{2,1,0:T(8,128)(2,1)} %copy-done.4), calls=%async_computation | async-start | bytes 1048576 | tf_op jit(solution)/shard_map/all_to_all | solution.py:591
  81.5 2.9 %shard_map.116 = (f32[1,256,768]{2,1,0:T(8,128)S(1)}, f32[1,256,768]{2,1,0:T(8,128)S(1)}, f32[1,256,768]{2,1,0:T(8,128)S(1)}, f32[1,256,768]{2,1,0:T(8,128)S(1)}) custom-call(bf16[256,512]{1,0:T(8,128)(2,1)S(1)} %get-tuple-element.33.skt_ref, bf16[512,12288]{1,0:T(8,128)(2,1)} %bitcast.31), custom_call_target="tpu_custom_call" | custom-call | tf_op jit(solution)/shard_map/pallas_call | solution.py:197
  84.4 2.6 %shard_map.123 = bf16[1,256,768]{2,1,0:T(8,128)(2,1)} custom-call(f32[1,256,768]{2,1,0:T(8,128)S(1)} %get-tuple-element.41.share_ref, bf16[4,256,768]{2,1,0:T(8,128)(2,1)S(1)} %collective-permute-done.10.refs_0_.refs_4_, bf16[2,256,768]{2,1,0:T(8,128)(2,1)} %collective-permute-done.11.refs_5_.refs_1_), custom_call_target="tpu_custom_call" | custom-call | tf_op jit(solution)/shard_map/pallas_call | solution.py:221
  87.0 1.7 %collective-permute-start.13 = (bf16[1,256,768]{2,1,0:T(8,128)(2,1)}, bf16[1,256,768]{2,1,0:T(8,128)(2,1)}, u32[]{:S(2)}, u32[]{:S(2)}) collective-permute-start(bf16[1,256,768]{2,1,0:T(8,128)(2,1)} %shard_map.123), channel_id=1, source_target_pairs={{0,2},{1,3},{2,0},{3,1},{4,6},{5,7},{6,4},{7,5},{8,10},{9,11},{10,... | collective-permute-start | bytes 1179656 | tf_op jit(solution)/shard_map/ppermute | solution.py:478
  88.7 2.0 %shard_map.122 = bf16[1,256,768]{2,1,0:T(8,128)(2,1)} custom-call(f32[1,256,768]{2,1,0:T(8,128)S(1)} %get-tuple-element.40.share_ref, bf16[4,256,768]{2,1,0:T(8,128)(2,1)S(1)} %collective-permute-done.8.refs_0_.refs_1_, bf16[2,256,768]{2,1,0:T(8,128)(2,1)} %collective-permute-done.9.refs_2_.refs_1_), custom_call_target="tpu_custom_call" | custom-call | tf_op jit(solution)/shard_map/pallas_call | solution.py:221
  90.7 1.5 %collective-permute-start.12 = (bf16[1,256,768]{2,1,0:T(8,128)(2,1)}, bf16[1,256,768]{2,1,0:T(8,128)(2,1)}, u32[]{:S(2)}, u32[]{:S(2)}) collective-permute-start(bf16[1,256,768]{2,1,0:T(8,128)(2,1)} %shard_map.122), channel_id=1, source_target_pairs={{0,4},{1,5},{2,6},{3,7},{4,0},{5,1},{6,2},{7,3},{8,12},{9,13},{10,... | collective-permute-start | bytes 1179656 | tf_op jit(solution)/shard_map/ppermute | solution.py:478
  92.2 4.9 %all-to-all-done.x_ref = bf16[32,32,256]{2,1,0:T(8,128)(2,1)} async-done(((bf16[32,32,256]{2,1,0:T(8,128)(2,1)}), bf16[32,32,256]{2,1,0:T(8,128)(2,1)}, u32[]{:S(2)}, u32[]{:S(2)}) %all-to-all-start) | async-done | bytes 524320 | tf_op jit(solution)/shard_map/all_to_all | solution.py:591
  97.1 2.0 %shard_map.129 = bf16[256,1024]{1,0:T(8,128)(2,1)} custom-call(bf16[32,32,256]{2,1,0:T(8,128)(2,1)} %all-to-all-done.x_ref), custom_call_target="tpu_custom_call" | custom-call | tf_op jit(solution)/shard_map/pallas_call | solution.py:365
  99.1 1.1 %copy-done.6 = f32[1,256,768]{2,1,0:T(8,128)S(1)} copy-done((f32[1,256,768]{2,1,0:T(8,128)S(1)}, f32[1,256,768]{2,1,0:T(8,128)}, u32[]{:S(2)}) %copy-start.6) | copy-done | bytes 786456
  100.2 1.1 %copy-done.8 = f32[1,256,768]{2,1,0:T(8,128)S(1)} copy-done((f32[1,256,768]{2,1,0:T(8,128)S(1)}, f32[1,256,768]{2,1,0:T(8,128)}, u32[]{:S(2)}) %copy-start.8) | copy-done | bytes 786456
  101.3 0.9 copy-done.11
  102.3 2.7 %shard_map.121.early_ref = f32[2,256,768]{2,1,0:T(8,128)S(1)} custom-call(f32[256,256]{1,0:T(8,128)S(1)} %copy-done.3, f32[256,256]{1,0:T(8,128)S(1)} %copy-done.11, bf16[256,1536]{1,0:T(8,128)(2,1)S(1)} %bitcast.19, f32[1,256,768]{2,1,0:T(8,128)S(1)} %copy-done.6, bf16[4,256,768]{2,1,0:T(8,128)(2,1)S(1)} %collective-permute-done.8.refs_0_.refs_1_, ...), custom_call_target="tpu_custom_call" | custom-call | tf_op jit(solution)/shard_map/pallas_call | solution.py:252
  105.1 2.7 %shard_map.124 = bf16[1536,256]{1,0:T(8,128)(2,1)} custom-call(f32[256,256]{1,0:T(8,128)S(1)} %copy-done.3, f32[2,256,768]{2,1,0:T(8,128)S(1)} %shard_map.121.early_ref, bf16[1,256,768]{2,1,0:T(8,128)(2,1)} %collective-permute-done.12.refs_0_, bf16[1,256,768]{2,1,0:T(8,128)(2,1)} %collective-permute-done.13.refs_1_), custom_call_target="tpu_custom_call" | custom-call | tf_op jit(solution)/shard_map/pallas_call | solution.py:273
  (52 shorter events, 1.1 us)
Async XLA Ops:
  0.6 53.3 %copy-start = (s32[4,16]{1,0:T(4,128)S(1)}, s32[4,16]{1,0:T(4,128)}, u32[]{:S(2)}) copy-start(s32[4,16]{1,0:T(4,128)} %param.15) | copy-start | bytes 772
  0.7 14.4 %copy-start.9 = (bf16[1,512,256]{2,1,0:T(8,128)(2,1)S(1)}, bf16[1,512,256]{2,1,0:T(8,128)(2,1)}, u32[]{:S(2)}) copy-start(bf16[1,512,256]{2,1,0:T(8,128)(2,1)} %param.9) | copy-start | bytes 786436
  0.7 14.4 %copy-start.12 = (bf16[1,256,256]{2,1,0:T(8,128)(2,1)S(1)}, bf16[1,256,256]{2,1,0:T(8,128)(2,1)}, u32[]{:S(2)}) copy-start(bf16[1,256,256]{2,1,0:T(8,128)(2,1)} %param.10) | copy-start | bytes 393220
  2.5 1.5 %collective-permute-start = (f32[128,256]{1,0:T(8,128)S(1)}, f32[128,256]{1,0:T(8,128)S(1)}, u32[]{:S(2)}, u32[]{:S(2)}) collective-permute-start(f32[128,256]{1,0:T(8,128)S(1)} %dynamic-slice_bitcast_fusion), channel_id=1, source_target_pairs={{0,1},{1,0},{2,3},{3,2},{4,5},{5,4},{6,7},{7,6},{8,9},{9,8},{10,11... | collective-permute-start | bytes 393224 | tf_op jit(solution)/shard_map/ppermute | solution.py:478
  4.1 5.8 %collective-permute-start.1 = (f32[128,256]{1,0:T(8,128)S(1)}, f32[128,256]{1,0:T(8,128)S(1)}, u32[]{:S(2)}, u32[]{:S(2)}) collective-permute-start(f32[128,256]{1,0:T(8,128)S(1)} %bitcast_add_fusion), channel_id=1, source_target_pairs={{0,2},{1,5},{2,0},{3,7},{4,6},{5,1},{6,4},{7,3},{8,10},{9,13},{10,... | collective-permute-start | bytes 393224 | tf_op jit(solution)/shard_map/ppermute | solution.py:478
  9.9 5.1 %collective-permute-start.2 = (f32[128,256]{1,0:T(8,128)S(1)}, f32[128,256]{1,0:T(8,128)S(1)}, u32[]{:S(2)}, u32[]{:S(2)}) collective-permute-start(f32[128,256]{1,0:T(8,128)S(1)} %add.70), channel_id=1, source_target_pairs={{0,4},{1,3},{2,6},{3,1},{4,0},{5,7},{6,2},{7,5},{8,12},{9,11},{10,... | collective-permute-start | bytes 393224 | tf_op jit(solution)/shard_map/ppermute | solution.py:478
  15.0 10.7 %collective-permute-start.3 = (f32[128,256]{1,0:T(8,128)S(1)}, f32[128,256]{1,0:T(8,128)S(1)}, u32[]{:S(2)}, u32[]{:S(2)}) collective-permute-start(f32[128,256]{1,0:T(8,128)S(1)} %add.71.mine_ref), channel_id=1, source_target_pairs={{0,1},{1,0},{2,3},{3,2},{4,5},{5,4},{6,7},{7,6},{8,9},{9,8},{10,11... | collective-permute-start | bytes 393224 | tf_op jit(solution)/shard_map/ppermute | solution.py:478
  26.5 14.4 %copy-start.13 = (s32[1,2,256]{2,1,0:T(2,128)S(1)}, s32[1,2,256]{2,1,0:T(2,128)}, u32[]{:S(2)}) copy-start(s32[1,2,256]{2,1,0:T(2,128)} %param.14) | copy-start | bytes 6148
  32.4 15.7 %copy-start.15 = (s32[8]{0:T(128)S(1)}, s32[8]{0:T(128)}, u32[]{:S(2)}) copy-start(s32[8]{0:T(128)} %constant.64.clone) | copy-start | bytes 100
  32.4 25.9 %collective-permute-start.10 = (bf16[4,256,768]{2,1,0:T(8,128)(2,1)}, bf16[4,256,768]{2,1,0:T(8,128)(2,1)S(1)}, u32[]{:S(2)}, u32[]{:S(2)}) collective-permute-start(bf16[4,256,768]{2,1,0:T(8,128)(2,1)} %get-tuple-element.38), channel_id=1, source_target_pairs={{0,1},{1,0},{2,3},{3,2},{4,5},{5,4},{6,7},{7,6},{8,9},{9,8},{10,11... | collective-permute-start | bytes 4718600 | tf_op jit(solution)/shard_map/ppermute | solution.py:478
  33.0 28.4 %collective-permute-start.8 = (bf16[4,256,768]{2,1,0:T(8,128)(2,1)}, bf16[4,256,768]{2,1,0:T(8,128)(2,1)S(1)}, u32[]{:S(2)}, u32[]{:S(2)}) collective-permute-start(bf16[4,256,768]{2,1,0:T(8,128)(2,1)} %get-tuple-element.35), channel_id=1, source_target_pairs={{0,1},{1,0},{2,3},{3,2},{4,5},{5,4},{6,7},{7,6},{8,9},{9,8},{10,11... | collective-permute-start | bytes 4718600 | tf_op jit(solution)/shard_map/ppermute | solution.py:478
  33.0 5.8 %collective-permute-start.4 = (f32[128,512]{1,0:T(8,128)S(1)}, f32[128,512]{1,0:T(8,128)S(1)}, u32[]{:S(2)}, u32[]{:S(2)}) collective-permute-start(f32[128,512]{1,0:T(8,128)S(1)} %get-tuple-element.30), channel_id=1, source_target_pairs={{0,1},{1,0},{2,3},{3,2},{4,5},{5,4},{6,7},{7,6},{8,9},{9,8},{10,11... | collective-permute-start | bytes 786440 | tf_op jit(solution)/shard_map/ppermute | solution.py:478
  38.9 6.4 %collective-permute-start.5 = (f32[128,512]{1,0:T(8,128)S(1)}, f32[128,512]{1,0:T(8,128)S(1)}, u32[]{:S(2)}, u32[]{:S(2)}) collective-permute-start(f32[128,512]{1,0:T(8,128)S(1)} %add.72), channel_id=1, source_target_pairs={{0,2},{1,5},{2,0},{3,7},{4,6},{5,1},{6,4},{7,3},{8,10},{9,13},{10,... | collective-permute-start | bytes 786440 | tf_op jit(solution)/shard_map/ppermute | solution.py:478
  41.2 7.0 %collective-permute-start.14 = (bf16[4,1,2,32,256]{4,3,2,1,0:T(8,128)(2,1)S(1)}, bf16[4,1,2,32,256]{4,3,2,1,0:T(8,128)(2,1)S(1)}, u32[]{:S(2)}, u32[]{:S(2)}) collective-permute-start(bf16[4,1,2,32,256]{4,3,2,1,0:T(8,128)(2,1)S(1)} %bitcast.26), channel_id=1, source_target_pairs={{0,4},{1,5},{2,6},{3,7},{4,0},{5,1},{6,2},{7,3},{8,12},{9,13},{10,... | collective-permute-start | bytes 393224 | tf_op jit(solution)/shard_map/ppermute | solution.py:478
  46.0 6.7 %collective-permute-start.6 = (f32[128,512]{1,0:T(8,128)}, f32[128,512]{1,0:T(8,128)}, u32[]{:S(2)}, u32[]{:S(2)}) collective-permute-start(f32[128,512]{1,0:T(8,128)} %add.73), channel_id=1, source_target_pairs={{0,4},{1,3},{2,6},{3,1},{4,0},{5,7},{6,2},{7,5},{8,12},{9,11},{10,... | collective-permute-start | bytes 786440 | tf_op jit(solution)/shard_map/ppermute | solution.py:478
  48.8 8.0 %collective-permute-start.15 = (bf16[2,2,2,32,256]{4,3,2,1,0:T(8,128)(2,1)}, bf16[2,2,2,32,256]{4,3,2,1,0:T(8,128)(2,1)}, u32[]{:S(2)}, u32[]{:S(2)}) collective-permute-start(bf16[2,2,2,32,256]{4,3,2,1,0:T(8,128)(2,1)} %get-tuple-element.46), channel_id=1, source_target_pairs={{0,2},{1,3},{2,0},{3,1},{4,6},{5,7},{6,4},{7,5},{8,10},{9,11},{10,... | collective-permute-start | bytes 393224 | tf_op jit(solution)/shard_map/ppermute | solution.py:478
  53.8 11.3 %collective-permute-start.7 = (f32[128,512]{1,0:T(8,128)S(1)}, f32[128,512]{1,0:T(8,128)S(1)}, u32[]{:S(2)}, u32[]{:S(2)}) collective-permute-start(f32[128,512]{1,0:T(8,128)S(1)} %add.74.mine_ref), channel_id=1, source_target_pairs={{0,1},{1,0},{2,3},{3,2},{4,5},{5,4},{6,7},{7,6},{8,9},{9,8},{10,11... | collective-permute-start | bytes 786440 | tf_op jit(solution)/shard_map/ppermute | solution.py:478
  57.8 17.2 %collective-permute-start.16 = (bf16[1,4,2,32,256]{4,3,2,1,0:T(8,128)(2,1)S(1)}, bf16[1,4,2,32,256]{4,3,2,1,0:T(8,128)(2,1)S(1)}, u32[]{:S(2)}, u32[]{:S(2)}) collective-permute-start(bf16[1,4,2,32,256]{4,3,2,1,0:T(8,128)(2,1)S(1)} %get-tuple-element.48), channel_id=1, source_target_pairs={{0,1},{1,0},{2,3},{3,2},{4,5},{5,4},{6,7},{7,6},{8,9},{9,8},{10,11... | collective-permute-start | bytes 393224 | tf_op jit(solution)/shard_map/ppermute | solution.py:478
  59.3 25.1 %collective-permute-start.11 = (bf16[2,256,768]{2,1,0:T(8,128)(2,1)}, bf16[2,256,768]{2,1,0:T(8,128)(2,1)}, u32[]{:S(2)}, u32[]{:S(2)}) collective-permute-start(bf16[2,256,768]{2,1,0:T(8,128)(2,1)} %shard_map.120), channel_id=1, source_target_pairs={{0,4},{1,5},{2,6},{3,7},{4,0},{5,1},{6,2},{7,3},{8,12},{9,13},{10,... | collective-permute-start | bytes 2359304 | tf_op jit(solution)/shard_map/ppermute | solution.py:478
  61.3 3.5 %copy-start.14 = (s32[24]{0:T(128)S(1)}, s32[24]{0:T(128)}, u32[]{:S(2)}) copy-start(s32[24]{0:T(128)} %param.16) | copy-start | bytes 292
  62.4 26.3 %collective-permute-start.9 = (bf16[2,256,768]{2,1,0:T(8,128)(2,1)}, bf16[2,256,768]{2,1,0:T(8,128)(2,1)}, u32[]{:S(2)}, u32[]{:S(2)}) collective-permute-start(bf16[2,256,768]{2,1,0:T(8,128)(2,1)} %shard_map.119), channel_id=1, source_target_pairs={{0,2},{1,3},{2,0},{3,1},{4,6},{5,7},{6,4},{7,5},{8,10},{9,11},{10,... | collective-permute-start | bytes 2359304 | tf_op jit(solution)/shard_map/ppermute | solution.py:478
  74.2 0.7 copy-start.10
  75.9 0.7 copy-start.2
  76.6 0.8 copy-start.4
  77.4 19.7 %all-to-all-start = ((bf16[32,32,256]{2,1,0:T(8,128)(2,1)}), bf16[32,32,256]{2,1,0:T(8,128)(2,1)}, u32[]{:S(2)}, u32[]{:S(2)}) async-start(bf16[32,32,256]{2,1,0:T(8,128)(2,1)} %copy-done.4), calls=%async_computation | async-start | bytes 1048576 | tf_op jit(solution)/shard_map/all_to_all | solution.py:591
  84.4 2.6 %copy-start.5 = (f32[1,256,768]{2,1,0:T(8,128)}, f32[1,256,768]{2,1,0:T(8,128)S(1)}, u32[]{:S(2)}) copy-start(f32[1,256,768]{2,1,0:T(8,128)S(1)} %get-tuple-element.34.refs_0_) | copy-start | bytes 2359300
  84.4 2.6 %copy-start.7 = (f32[1,256,768]{2,1,0:T(8,128)}, f32[1,256,768]{2,1,0:T(8,128)S(1)}, u32[]{:S(2)}) copy-start(f32[1,256,768]{2,1,0:T(8,128)S(1)} %get-tuple-element.37.refs_3_) | copy-start | bytes 2359300
  87.0 18.0 %collective-permute-start.13 = (bf16[1,256,768]{2,1,0:T(8,128)(2,1)}, bf16[1,256,768]{2,1,0:T(8,128)(2,1)}, u32[]{:S(2)}, u32[]{:S(2)}) collective-permute-start(bf16[1,256,768]{2,1,0:T(8,128)(2,1)} %shard_map.123), channel_id=1, source_target_pairs={{0,2},{1,3},{2,0},{3,1},{4,6},{5,7},{6,4},{7,5},{8,10},{9,11},{10,... | collective-permute-start | bytes 1179656 | tf_op jit(solution)/shard_map/ppermute | solution.py:478
  88.7 10.4 %copy-start.3 = (f32[256,256]{1,0:T(8,128)S(1)}, f32[256,256]{1,0:T(8,128)}, u32[]{:S(2)}) copy-start(f32[256,256]{1,0:T(8,128)} %copy-done.2) | copy-start | bytes 786436
  90.7 14.3 %collective-permute-start.12 = (bf16[1,256,768]{2,1,0:T(8,128)(2,1)}, bf16[1,256,768]{2,1,0:T(8,128)(2,1)}, u32[]{:S(2)}, u32[]{:S(2)}) collective-permute-start(bf16[1,256,768]{2,1,0:T(8,128)(2,1)} %shard_map.122), channel_id=1, source_target_pairs={{0,4},{1,5},{2,6},{3,7},{4,0},{5,1},{6,2},{7,3},{8,12},{9,13},{10,... | collective-permute-start | bytes 1179656 | tf_op jit(solution)/shard_map/ppermute | solution.py:478
  97.1 2.0 %copy-start.1 = (bf16[1,256,1536]{2,1,0:T(8,128)(2,1)S(1)}, bf16[1,256,1536]{2,1,0:T(8,128)(2,1)}, u32[]{:S(2)}) copy-start(bf16[1,256,1536]{2,1,0:T(8,128)(2,1)} %param.11) | copy-start | bytes 2359300
  99.1 1.1 %copy-start.6 = (f32[1,256,768]{2,1,0:T(8,128)S(1)}, f32[1,256,768]{2,1,0:T(8,128)}, u32[]{:S(2)}) copy-start(f32[1,256,768]{2,1,0:T(8,128)} %copy-done.5) | copy-start | bytes 2359300
  100.2 1.1 %copy-start.8 = (f32[1,256,768]{2,1,0:T(8,128)S(1)}, f32[1,256,768]{2,1,0:T(8,128)}, u32[]{:S(2)}) copy-start(f32[1,256,768]{2,1,0:T(8,128)} %copy-done.7) | copy-start | bytes 2359300
  101.3 0.9 copy-start.11
